TPU v7x, 128 devices: a whole 4x4x4 slice. The times are simulated.
128 devices in a mesh: section: 4 (over z), dp: 8 (over y, core), mp: 4 (over x).
Axes of the slice: x: 4, y: 4, z: 4, core: 2. Of those that a mesh axis runs over, the one named last changes fastest.
Arguments:
- text: bfloat16 [4, 4096, 4096], P('section', ('dp', 'mp')), may hold values from -6 to 6
- patches: bfloat16 [16384, 1024], P(('section', 'dp')), may hold values from -6 to 6
- segments: int32 [4, 8, 512], P('section', 'dp'), may hold values from 0 to 3, never falling along the last dimension, each value on 1 to 256 neighbouring positions
- loss_mask: int32 [4, 4096], P('section', ('dp', 'mp')), may hold values from 0 to 1, as said below
- tile_batch: int32 [8, 8], P('dp'), may hold values from 0 to 3, as said below
- tile_offset: int32 [8, 8], P('dp'), may hold values from 0 to 448, as said below
- attn_gain: float32 [4, 4096], P('section'), may hold values from 0.5 to 2
- w_query: bfloat16 [4, 4096, 2048], P('section', None, 'mp'), may hold values from -0.09375 to 0.09375
- w_kv: bfloat16 [4, 2, 4096, 512], P('section', None, None, 'mp'), may hold values from -0.09375 to 0.09375
- w_out: bfloat16 [4, 2048, 4096], P('section', 'mp'), may hold values from -0.125 to 0.125
- vis_gain: float32 [2, 1024], replicated, may hold values from 0.5 to 2
- vis_bias: float32 [2, 1024], replicated, may hold values from -3 to 3
- v_qkv: bfloat16 [3, 1024, 1024], P(None, ('section', 'dp'), 'mp'), may hold values from -0.1875 to 0.1875
- v_out: bfloat16 [1024, 1024], P('mp', ('section', 'dp')), may hold values from -0.1875 to 0.1875
- v_up: bfloat16 [1024, 4096], P(('section', 'dp'), 'mp'), may hold values from -0.1875 to 0.1875
- v_down: bfloat16 [4096, 1024], P('mp', ('section', 'dp')), may hold values from -0.09375 to 0.09375
- v_proj: bfloat16 [4096, 4096], P(('section', 'dp'), 'mp'), may hold values from -0.09375 to 0.09375
Outputs:
- hidden: bfloat16 [4, 4096, 4096], P('section', ('dp', 'mp'))
- token_weight: float32 [4, 4096], P('section', ('dp', 'mp'))
Inputs may be any that keep to these rules, and one draw needn't show every extreme that they name: `tile_batch`: in every data-parallel index, the 2 tiles of each section index go 1 to each of two different micro-batches; one micro-batch receives 1 tiles from every section index. `tile_offset`: offsets are multiples of 64; the runs of one sequence never intersect. `loss_mask`: the first position of every sequence is a one.
All inputs are finite; a program needn't handle non-finite values.
Results may differ from a plain program's by a relative error of at most 0.025.
Values may be sent and summed in bfloat16 or wider, within the bound.
A program may use at most 192 MiB of HBM per device.

v0:
```python
import jax
import jax.numpy as jnp
from jax import lax
from jax.sharding import Mesh
from jax.sharding import PartitionSpec as P

HD = 128
VHD = 64
GRID = 16
PATCH = 256
POOL = 64
SECTION_DP = ("section", "dp_0", "dp_1")
SECTION_DP_MP = ("section", "dp_0", "dp_1", "mp")
DP = ("dp_0", "dp_1")
DP_MP = ("dp_0", "dp_1", "mp")
EPS = 1e-05
ROPE_BASE = 500000.0
BLOCKED = -1e30


def copy_for_each(array, axis):
    copies = jnp.broadcast_to(array, (lax.axis_size(axis), *array.shape))
    return lax.all_to_all(copies, axis, split_axis=0, concat_axis=0, tiled=True)


def over_copies(array, axis):
    everything = copy_for_each(array, axis)
    return jnp.sum(everything.astype(jnp.float32), axis=0)


def laid_out(tiles, dim):
    lengths = list(tiles.shape[1:])
    lengths[dim] *= tiles.shape[0]
    return jnp.moveaxis(tiles, 0, dim).reshape(lengths)


def one_gather(arrays, axis, dims):
    flat = jnp.concatenate([a.reshape(-1) for a in arrays])
    lines, at, done = (lax.all_gather(flat, axis), 0, [])
    for a, dim in zip(arrays, dims):
        tiles = lines[:, at : at + a.size].reshape(-1, *a.shape)
        done.append(laid_out(tiles, dim))
        at += a.size
    return tuple(done)


def shifted(value, axis, steps):
    count = lax.axis_size(axis)
    pairs = [(source, (source + steps) % count) for source in range(count)]
    return lax.ppermute(value, axis, pairs)


def over_axes(array, axes):
    for axis in axes:
        array = lax.psum(array, axis)
    return array


def layer_norm(values, gain, bias):
    wide = values.astype(jnp.float32)
    center = wide - jnp.mean(wide, axis=-1, keepdims=True)
    spread = jnp.mean(center * center, axis=-1, keepdims=True)
    return (center * lax.rsqrt(spread + EPS) * gain + bias).astype(jnp.bfloat16)


def rms_norm(values, gain):
    wide = values.astype(jnp.float32)
    power = jnp.mean(wide * wide, axis=-1, keepdims=True)
    return (wide * lax.rsqrt(power + EPS) * gain).astype(jnp.bfloat16)


def rotate(values, positions):
    half_width = values.shape[-1] // 2
    freqs = ROPE_BASE ** (-2.0 * jnp.arange(half_width, dtype=jnp.float32) / values.shape[-1])
    angles = positions.astype(jnp.float32)[:, None] * freqs[None, :]
    cosine = jnp.cos(angles)[:, None, :]
    sinus_part = jnp.sin(angles)[:, None, :]
    first_half = values[..., :half_width]
    second_half = values[..., half_width:]
    return jnp.concatenate(
        [
            first_half * cosine - second_half * sinus_part,
            second_half * cosine + first_half * sinus_part,
        ],
        axis=-1,
    )


def pixel_shuffle(states):
    tile_count = states.shape[0] // PATCH
    side_half = GRID // 2
    width = states.shape[1]
    arranged = states.reshape(tile_count, side_half, 2, side_half, 2, width)
    return arranged.transpose(0, 1, 3, 2, 4, 5).reshape(
        tile_count * side_half * side_half, 4 * width
    )


def block_sum(partial_value):
    return over_copies(partial_value.astype(jnp.bfloat16), "mp").astype(jnp.float32)


def encode_tiles(patches, vis_gain, vis_bias, qkv_full, out_full, up_full, down_full, proj_full):
    tile_count = patches.shape[0] // PATCH
    local_width = qkv_full.shape[2]
    head_count = local_width // VHD
    normed = layer_norm(patches, vis_gain[0], vis_bias[0])
    projected = [
        jnp.dot(normed, qkv_full[index], preferred_element_type=jnp.float32)
        .astype(jnp.bfloat16)
        .reshape(tile_count, PATCH, head_count, VHD)
        for index in range(3)
    ]
    scores = jnp.einsum(
        "tqhd,tkhd->thqk", projected[0], projected[1], preferred_element_type=jnp.float32
    ) * VHD ** (-0.5)
    probs = jax.nn.softmax(scores, axis=-1).astype(jnp.bfloat16)
    mixed = (
        jnp.einsum("thqk,tkhd->tqhd", probs, projected[2], preferred_element_type=jnp.float32)
        .astype(jnp.bfloat16)
        .reshape(tile_count * PATCH, local_width)
    )
    attended = block_sum(jnp.dot(mixed, out_full, preferred_element_type=jnp.float32))
    residual = (patches.astype(jnp.float32) + attended).astype(jnp.bfloat16)
    normed_two = layer_norm(residual, vis_gain[1], vis_bias[1])
    inner = jax.nn.gelu(
        jnp.dot(normed_two, up_full, preferred_element_type=jnp.float32), approximate=False
    ).astype(jnp.bfloat16)
    fed = block_sum(jnp.dot(inner, down_full, preferred_element_type=jnp.float32))
    states = (residual.astype(jnp.float32) + fed).astype(jnp.bfloat16)
    return jnp.dot(pixel_shuffle(states), proj_full, preferred_element_type=jnp.float32).astype(
        jnp.bfloat16
    )


def decoder_layer(active, state, segment_ids, gain, w_query, w_kv, w_out):
    normed = rms_norm(state, gain)
    query_width = w_query.shape[1]
    pair_width = w_kv.shape[2]
    joined_width = query_width + 2 * pair_width
    model_width = w_out.shape[1]
    piece = lax.all_gather(normed, "mp", axis=0, tiled=True)
    row_count = piece.shape[0]

    def project_computed(rows):
        positions = jnp.arange(row_count, dtype=jnp.int32)
        query = jnp.dot(rows, w_query, preferred_element_type=jnp.float32).reshape(
            row_count, query_width // HD, HD
        )
        keyed = jnp.dot(rows, w_kv[0], preferred_element_type=jnp.float32).reshape(
            row_count, pair_width // HD, HD
        )
        valued = jnp.dot(rows, w_kv[1], preferred_element_type=jnp.float32)
        return jnp.concatenate(
            [
                rotate(query, positions).reshape(row_count, query_width),
                rotate(keyed, positions).reshape(row_count, pair_width),
                valued,
            ],
            axis=1,
        ).astype(jnp.bfloat16)

    def project_skipped(rows):
        return jnp.zeros((row_count, joined_width), jnp.bfloat16)

    joined = lax.cond(active, project_computed, project_skipped, piece)
    length = joined.shape[0]
    pair_heads = pair_width // HD
    group_size = query_width // pair_width

    def attend(joined_rows):
        query = joined_rows[:, :query_width].reshape(length, pair_heads, group_size, HD)
        keyed = joined_rows[:, query_width : query_width + pair_width].reshape(
            length, pair_heads, HD
        )
        valued = joined_rows[:, query_width + pair_width :].reshape(length, pair_heads, HD)
        scores = jnp.einsum(
            "qkgd,skd->kgqs", query, keyed, preferred_element_type=jnp.float32
        ) * HD ** (-0.5)
        row_ids = jnp.arange(length, dtype=jnp.int32)
        allowed = (segment_ids[:, None] == segment_ids[None, :]) & (
            row_ids[None, :] <= row_ids[:, None]
        )
        scores = jnp.where(allowed, scores, BLOCKED)
        probs = jax.nn.softmax(scores, axis=-1).astype(jnp.bfloat16)
        return (
            jnp.einsum("kgqs,skd->qkgd", probs, valued, preferred_element_type=jnp.float32)
            .astype(jnp.bfloat16)
            .reshape(length, query_width)
        )

    def attend_skipped(joined_rows):
        return jnp.zeros((length, query_width), jnp.bfloat16)

    mixed = lax.cond(active, attend, attend_skipped, joined)
    count = state.shape[0] * lax.axis_size("mp")

    def out_computed(values):
        return jnp.dot(values, w_out, preferred_element_type=jnp.float32)

    def out_skipped(values):
        return jnp.zeros((count, model_width), jnp.float32)

    summed = lax.psum_scatter(
        lax.cond(active, out_computed, out_skipped, mixed).astype(jnp.bfloat16),
        "mp",
        scatter_dimension=0,
        tiled=True,
    ).astype(jnp.float32)
    updated = (state.astype(jnp.float32) + summed).astype(jnp.bfloat16)
    return jnp.where(active, updated, state)


def shards(
    text,
    patches,
    segments,
    loss_mask,
    tile_batch,
    tile_offset,
    attn_gain,
    w_query,
    w_kv,
    w_out,
    vis_gain,
    vis_bias,
    v_qkv,
    v_out,
    v_up,
    v_down,
    v_proj,
):
    sections = lax.axis_size("section")
    section_at = lax.axis_index("section")
    part_at = lax.axis_index("mp")
    qkv_full, out_full, up_full, down_full, proj_full = one_gather(
        (v_qkv, v_out, v_up, v_down, v_proj), SECTION_DP, (1, 1, 0, 1, 0)
    )
    embedded = encode_tiles(
        patches, vis_gain, vis_bias, qkv_full, out_full, up_full, down_full, proj_full
    )
    length = segments.shape[2]
    tiles_here = embedded.shape[0] // POOL
    batch_all = tile_batch[0]
    offset_all = tile_offset[0]
    own_batch = lax.dynamic_slice_in_dim(batch_all, section_at * tiles_here, tiles_here, 0)
    capacity = tiles_here // 2
    block_rows = capacity * POOL
    local_ids = jnp.arange(tiles_here, dtype=jnp.int32)
    local_same = (own_batch[:, None] == own_batch[None, :]) & (
        local_ids[None, :] < local_ids[:, None]
    )
    local_rank = jnp.sum(local_same.astype(jnp.int32), axis=1)
    send_rows = jnp.arange(sections * block_rows, dtype=jnp.int32)
    send_target = send_rows // block_rows
    send_rank = send_rows % block_rows // POOL
    send_match = (own_batch[None, :] == send_target[:, None]) & (
        local_rank[None, :] == send_rank[:, None]
    )
    own_rows = jnp.arange(tiles_here * POOL, dtype=jnp.int32)
    send_pick = jnp.repeat(send_match, POOL, axis=1) & (
        (own_rows % POOL)[None, :] == (send_rows % POOL)[:, None]
    )
    blocks = jnp.dot(
        send_pick.astype(jnp.bfloat16), embedded, preferred_element_type=jnp.float32
    ).astype(jnp.bfloat16)
    arrived = lax.all_to_all(blocks, "section", split_axis=0, concat_axis=0, tiled=True)
    tile_ids = jnp.arange(batch_all.shape[0], dtype=jnp.int32)
    source_ids = tile_ids // tiles_here
    tile_same = (
        (batch_all[:, None] == batch_all[None, :])
        & (source_ids[:, None] == source_ids[None, :])
        & (tile_ids[None, :] < tile_ids[:, None])
    )
    tile_rank = jnp.sum(tile_same.astype(jnp.int32), axis=1)
    slot_rows = jnp.arange(sections * block_rows, dtype=jnp.int32)
    slot_source = slot_rows // block_rows
    slot_rank = slot_rows % block_rows // POOL
    match = (
        (batch_all[None, :] == section_at)
        & (source_ids[None, :] == slot_source[:, None])
        & (tile_rank[None, :] == slot_rank[:, None])
    )
    slot_place = jnp.sum(match.astype(jnp.int32) * offset_all[None, :], axis=1) + slot_rows % POOL
    slot_valid = jnp.any(match, axis=1)
    places = jnp.arange(length, dtype=jnp.int32)
    picker = ((places[:, None] == slot_place[None, :]) & slot_valid[None, :]).astype(jnp.bfloat16)
    image_cols = jnp.dot(picker, arrived, preferred_element_type=jnp.float32).astype(jnp.bfloat16)
    image_rows = lax.all_to_all(image_cols, "mp", split_axis=0, concat_axis=1, tiled=True)
    shard_rows = image_rows.shape[0]
    positions = part_at * shard_rows + jnp.arange(shard_rows, dtype=jnp.int32)
    covered = jnp.any(
        (batch_all[None, :] == section_at)
        & (positions[:, None] >= offset_all[None, :])
        & (positions[:, None] < offset_all[None, :] + POOL),
        axis=1,
    )
    start_state = jnp.where(covered[:, None], image_rows, text[0])
    gain_here = attn_gain[0]
    query_here = w_query[0]
    pair_here = w_kv[0]
    out_here = w_out[0]
    state = start_state
    segment_ids = segments[0, 0]
    for tick_index in range(2 * sections):
        if tick_index < 2 * sections - 1:
            micro_at = jnp.mod(section_at - tick_index, sections)
            begin_at = jnp.mod(sections - micro_at, sections)
            active = (tick_index >= begin_at) & (tick_index < begin_at + sections)
            state = decoder_layer(
                active, state, segment_ids, gain_here, query_here, pair_here, out_here
            )
        state, segment_ids = shifted((state, segment_ids), "section", 1)
    totals = over_axes(jnp.sum(loss_mask), SECTION_DP_MP)
    scaling = float(sections * lax.axis_size(DP) * length)
    token_weight = loss_mask.astype(jnp.float32) * scaling / totals.astype(jnp.float32)
    return (state[None], token_weight)


def solution(mesh):
    split = Mesh(
        mesh.devices.reshape(mesh.shape["section"], 4, 2, mesh.shape["mp"]),
        ("section", "dp_0", "dp_1", "mp"),
    )
    return jax.shard_map(
        shards,
        mesh=split,
        in_specs=(
            P("section", DP_MP, None),
            P(SECTION_DP, None),
            P("section", DP, None),
            P("section", DP_MP),
            P(DP, None),
            P(DP, None),
            P("section", None),
            P("section", None, "mp"),
            P("section", None, None, "mp"),
            P("section", "mp", None),
            P(),
            P(),
            P(None, SECTION_DP, "mp"),
            P("mp", SECTION_DP),
            P(SECTION_DP, "mp"),
            P("mp", SECTION_DP),
            P(SECTION_DP, "mp"),
        ),
        out_specs=(P("section", DP_MP, None), P("section", DP_MP)),
        check_vma=False,
    )
```

profile of v0, /device:TPU:32, one launch (start us, length us, event | category | flops | bytes accessed | tf_op | source)
XLA Modules:
  0.0 1387.6 jit_solution(4361427265575410445)
XLA Ops:
  16.4 66.2 %all-gather.24.cloned.1.call-done = bf16[7340032]{0:T(1024)(128)(2,1)} async-done(((bf16[229376]{0:T(1024)(128)(2,1)}), bf16[7340032]{0:T(1024)(128)(2,1)}) %all-gather.24.cloned.1.call-update) | async-done | bytes 14680080 | tf_op jit(solution)/shard_map/all_gather | solution.py:39
  82.6 13.2 reshape.1320
  141.0 27.2 %all-to-all-done = bf16[4,512,1024]{2,1,0:T(8,128)(2,1)} async-done(((bf16[4,512,1024]{2,1,0:T(8,128)(2,1)}), bf16[4,512,1024]{2,1,0:T(8,128)(2,1)}, u32[]{:S(2)}, u32[]{:S(2)}) %all-to-all-start) | async-done | bytes 4194336 | tf_op jit(solution)/shard_map/all_to_all | solution.py:23
  205.8 31.9 %all-to-all-done.1 = bf16[4,512,1024]{2,1,0:T(8,128)(2,1)} async-done(((bf16[4,512,1024]{2,1,0:T(8,128)(2,1)}), bf16[4,512,1024]{2,1,0:T(8,128)(2,1)}, u32[]{:S(2)}, u32[]{:S(2)}) %all-to-all-start.1) | async-done | bytes 4194336 | tf_op jit(solution)/shard_map/all_to_all | solution.py:23
  268.5 11.0 all-to-all-done.3
  285.6 46.9 %all-gather.10.cloned.1.call-done = bf16[512,4096]{1,0:T(8,128)(2,1)} async-done(((bf16[128,4096]{1,0:T(8,128)(2,1)}), bf16[512,4096]{1,0:T(8,128)(2,1)}) %all-gather.10.cloned.1.call-update) | async-done | bytes 4194320 | tf_op jit(solution)/shard_map/all_gather | solution.py:142
  341.9 62.8 %reduce-scatter.8.cloned.1.call-done = bf16[128,4096]{1,0:T(8,128)(2,1)} async-done(((bf16[512,4096]{1,0:T(8,128)(2,1)}), bf16[128,4096]{1,0:T(8,128)(2,1)}) %reduce-scatter.8.cloned.1.call-update) | async-done | bytes 1048592 | tf_op jit(solution)/shard_map/reduce_scatter | solution.py:204
  408.5 23.3 %collective-permute-done = bf16[128,4096]{1,0:T(8,128)(2,1)S(1)} collective-permute-done((bf16[128,4096]{1,0:T(8,128)(2,1)S(1)}, bf16[128,4096]{1,0:T(8,128)(2,1)S(1)}, u32[]{:S(2)}, u32[]{:S(2)}) %collective-permute-start) | collective-permute-done | bytes 1048608 | tf_op jit(solution)/shard_map/ppermute | solution.py:50
  435.0 46.4 %all-gather.12.cloned.1.call-done = bf16[512,4096]{1,0:T(8,128)(2,1)} async-done(((bf16[128,4096]{1,0:T(8,128)(2,1)}), bf16[512,4096]{1,0:T(8,128)(2,1)}) %all-gather.12.cloned.1.call-update) | async-done | bytes 4194320 | tf_op jit(solution)/shard_map/all_gather | solution.py:142
  491.6 10.4 conditional.25
  509.2 45.7 %reduce-scatter.10.cloned.1.call-done = bf16[128,4096]{1,0:T(8,128)(2,1)} async-done(((bf16[512,4096]{1,0:T(8,128)(2,1)}), bf16[128,4096]{1,0:T(8,128)(2,1)}) %reduce-scatter.10.cloned.1.call-update) | async-done | bytes 1048592 | tf_op jit(solution)/shard_map/reduce_scatter | solution.py:204
  558.0 23.3 %collective-permute-done.2 = bf16[128,4096]{1,0:T(8,128)(2,1)S(1)} collective-permute-done((bf16[128,4096]{1,0:T(8,128)(2,1)S(1)}, bf16[128,4096]{1,0:T(8,128)(2,1)S(1)}, u32[]{:S(2)}, u32[]{:S(2)}) %collective-permute-start.2) | collective-permute-done | bytes 1048608 | tf_op jit(solution)/shard_map/ppermute | solution.py:50
  584.6 46.4 %all-gather.14.cloned.1.call-done = bf16[512,4096]{1,0:T(8,128)(2,1)} async-done(((bf16[128,4096]{1,0:T(8,128)(2,1)}), bf16[512,4096]{1,0:T(8,128)(2,1)}) %all-gather.14.cloned.1.call-update) | async-done | bytes 4194320 | tf_op jit(solution)/shard_map/all_gather | solution.py:142
  641.2 10.6 conditional.28
  658.6 47.3 %reduce-scatter.12.cloned.1.call-done = bf16[128,4096]{1,0:T(8,128)(2,1)} async-done(((bf16[512,4096]{1,0:T(8,128)(2,1)}), bf16[128,4096]{1,0:T(8,128)(2,1)}) %reduce-scatter.12.cloned.1.call-update) | async-done | bytes 1048592 | tf_op jit(solution)/shard_map/reduce_scatter | solution.py:204
  709.0 23.3 %collective-permute-done.4 = bf16[128,4096]{1,0:T(8,128)(2,1)S(1)} collective-permute-done((bf16[128,4096]{1,0:T(8,128)(2,1)S(1)}, bf16[128,4096]{1,0:T(8,128)(2,1)S(1)}, u32[]{:S(2)}, u32[]{:S(2)}) %collective-permute-start.4) | collective-permute-done | bytes 1048608 | tf_op jit(solution)/shard_map/ppermute | solution.py:50
  735.6 46.4 %all-gather.16.cloned.1.call-done = bf16[512,4096]{1,0:T(8,128)(2,1)} async-done(((bf16[128,4096]{1,0:T(8,128)(2,1)}), bf16[512,4096]{1,0:T(8,128)(2,1)}) %all-gather.16.cloned.1.call-update) | async-done | bytes 4194320 | tf_op jit(solution)/shard_map/all_gather | solution.py:142
  782.0 10.4 conditional.30
  792.3 10.5 conditional.31
  810.0 46.8 %reduce-scatter.14.cloned.1.call-done = bf16[128,4096]{1,0:T(8,128)(2,1)} async-done(((bf16[512,4096]{1,0:T(8,128)(2,1)}), bf16[128,4096]{1,0:T(8,128)(2,1)}) %reduce-scatter.14.cloned.1.call-update) | async-done | bytes 1048592 | tf_op jit(solution)/shard_map/reduce_scatter | solution.py:204
  860.0 23.3 %collective-permute-done.6 = bf16[128,4096]{1,0:T(8,128)(2,1)S(1)} collective-permute-done((bf16[128,4096]{1,0:T(8,128)(2,1)S(1)}, bf16[128,4096]{1,0:T(8,128)(2,1)S(1)}, u32[]{:S(2)}, u32[]{:S(2)}) %collective-permute-start.6) | collective-permute-done | bytes 1048608 | tf_op jit(solution)/shard_map/ppermute | solution.py:50
  886.6 46.4 %all-gather.18.cloned.1.call-done = bf16[512,4096]{1,0:T(8,128)(2,1)} async-done(((bf16[128,4096]{1,0:T(8,128)(2,1)}), bf16[512,4096]{1,0:T(8,128)(2,1)}) %all-gather.18.cloned.1.call-update) | async-done | bytes 4194320 | tf_op jit(solution)/shard_map/all_gather | solution.py:142
  943.1 10.5 conditional.34
  960.5 47.3 %reduce-scatter.16.cloned.1.call-done = bf16[128,4096]{1,0:T(8,128)(2,1)} async-done(((bf16[512,4096]{1,0:T(8,128)(2,1)}), bf16[128,4096]{1,0:T(8,128)(2,1)}) %reduce-scatter.16.cloned.1.call-update) | async-done | bytes 1048592 | tf_op jit(solution)/shard_map/reduce_scatter | solution.py:204
  1011.0 23.3 %collective-permute-done.8 = bf16[128,4096]{1,0:T(8,128)(2,1)S(1)} collective-permute-done((bf16[128,4096]{1,0:T(8,128)(2,1)S(1)}, bf16[128,4096]{1,0:T(8,128)(2,1)S(1)}, u32[]{:S(2)}, u32[]{:S(2)}) %collective-permute-start.8) | collective-permute-done | bytes 1048608 | tf_op jit(solution)/shard_map/ppermute | solution.py:50
  1037.5 46.4 %all-gather.20.cloned.1.call-done = bf16[512,4096]{1,0:T(8,128)(2,1)} async-done(((bf16[128,4096]{1,0:T(8,128)(2,1)}), bf16[512,4096]{1,0:T(8,128)(2,1)}) %all-gather.20.cloned.1.call-update) | async-done | bytes 4194320 | tf_op jit(solution)/shard_map/all_gather | solution.py:142
  1088.5 70.3 %reduce-scatter.18.cloned.1.call-done = bf16[128,4096]{1,0:T(8,128)(2,1)} async-done(((bf16[512,4096]{1,0:T(8,128)(2,1)}), bf16[128,4096]{1,0:T(8,128)(2,1)}) %reduce-scatter.18.cloned.1.call-update) | async-done | bytes 1048592 | tf_op jit(solution)/shard_map/reduce_scatter | solution.py:204
  1161.9 23.3 %collective-permute-done.10 = bf16[128,4096]{1,0:T(8,128)(2,1)S(1)} collective-permute-done((bf16[128,4096]{1,0:T(8,128)(2,1)S(1)}, bf16[128,4096]{1,0:T(8,128)(2,1)S(1)}, u32[]{:S(2)}, u32[]{:S(2)}) %collective-permute-start.10) | collective-permute-done | bytes 1048608 | tf_op jit(solution)/shard_map/ppermute | solution.py:50
  1188.5 46.4 %all-gather.22.cloned.1.call-done = bf16[512,4096]{1,0:T(8,128)(2,1)} async-done(((bf16[128,4096]{1,0:T(8,128)(2,1)}), bf16[512,4096]{1,0:T(8,128)(2,1)}) %all-gather.22.cloned.1.call-update) | async-done | bytes 4194320 | tf_op jit(solution)/shard_map/all_gather | solution.py:142
  1237.8 65.9 %reduce-scatter.20.cloned.1.call-done = bf16[128,4096]{1,0:T(8,128)(2,1)} async-done(((bf16[512,4096]{1,0:T(8,128)(2,1)}), bf16[128,4096]{1,0:T(8,128)(2,1)}) %reduce-scatter.20.cloned.1.call-update) | async-done | bytes 1048592 | tf_op jit(solution)/shard_map/reduce_scatter | solution.py:204
  1306.9 23.3 %collective-permute-done.12 = bf16[128,4096]{1,0:T(8,128)(2,1)S(1)} collective-permute-done((bf16[128,4096]{1,0:T(8,128)(2,1)S(1)}, bf16[128,4096]{1,0:T(8,128)(2,1)S(1)}, u32[]{:S(2)}, u32[]{:S(2)}) %collective-permute-start.12) | collective-permute-done | bytes 1048608 | tf_op jit(solution)/shard_map/ppermute | solution.py:50
  1332.3 26.3 %psum.28 = s32[]{:T(128)} all-reduce(s32[]{:T(128)} %reduce_sum.242), channel_id=1, replica_groups=mesh['section'=4,'dp_0'=4,'dp_1'=2,'mp'=4] {'section'}, use_global_device_ids=true, to_apply=%region_84.85 | all-reduce | flops 1 | bytes 8 | tf_op jit(solution)/shard_map/psum | solution.py:55
  (310 shorter events, 389.6 us)
Async XLA Ops:
  7.2 75.4 %all-gather.24.cloned.1.call-start = ((), (), s32[]{:S(2)}) async-start(), calls=%async_computation.25 | async-start | bytes 15138816 | tf_op jit(solution)/shard_map/all_gather | solution.py:39
  113.6 54.6 %all-to-all-start = ((bf16[4,512,1024]{2,1,0:T(8,128)(2,1)}), bf16[4,512,1024]{2,1,0:T(8,128)(2,1)}, u32[]{:S(2)}, u32[]{:S(2)}) async-start(bf16[4,512,1024]{2,1,0:T(8,128)(2,1)} %broadcast_in_dim.76), calls=%async_computation | async-start | bytes 8388608 | tf_op jit(solution)/shard_map/all_to_all | solution.py:23
  183.6 54.1 %all-to-all-start.1 = ((bf16[4,512,1024]{2,1,0:T(8,128)(2,1)}), bf16[4,512,1024]{2,1,0:T(8,128)(2,1)}, u32[]{:S(2)}, u32[]{:S(2)}) async-start(bf16[4,512,1024]{2,1,0:T(8,128)(2,1)} %broadcast_in_dim.85), calls=%async_computation.1 | async-start | bytes 8388608 | tf_op jit(solution)/shard_map/all_to_all | solution.py:23
  262.4 17.1 %all-to-all-start.3 = ((bf16[4,128,1024]{2,1,0:T(8,128)(2,1)}), bf16[4,128,1024]{2,1,0:T(8,128)(2,1)}, u32[]{:S(2)}, u32[]{:S(2)}) async-start(bf16[4,128,1024]{2,1,0:T(8,128)(2,1)} %bitcast.135), calls=%async_computation.3 | async-start | bytes 2097152 | tf_op jit(solution)/shard_map/all_to_all | solution.py:289
  266.8 65.7 %all-gather.10.cloned.1.call-start = ((), (), s32[]{:S(2)}) async-start(), calls=%async_computation.11 | async-start | bytes 5242880 | tf_op jit(solution)/shard_map/all_gather | solution.py:142
  285.5 119.2 %reduce-scatter.8.cloned.1.call-start = ((), (), s32[]{:S(2)}) async-start(), calls=%async_computation.12 | async-start | bytes 5242880 | tf_op jit(solution)/shard_map/reduce_scatter | solution.py:204
  336.9 144.5 %all-gather.12.cloned.1.call-start = ((), (), s32[]{:S(2)}) async-start(), calls=%async_computation.13 | async-start | bytes 5242880 | tf_op jit(solution)/shard_map/all_gather | solution.py:142
  406.8 24.9 %collective-permute-start = (bf16[128,4096]{1,0:T(8,128)(2,1)S(1)}, bf16[128,4096]{1,0:T(8,128)(2,1)S(1)}, u32[]{:S(2)}, u32[]{:S(2)}) collective-permute-start(bf16[128,4096]{1,0:T(8,128)(2,1)S(1)} %fusion.241), channel_id=1, source_target_pairs={{0,32},{32,64},{64,96},{96,0},{1,33},{33,65},{65,97},{97,1},{2,34}... | collective-permute-start | bytes 3145736 | tf_op jit(solution)/shard_map/ppermute | solution.py:50
  433.4 121.5 %reduce-scatter.10.cloned.1.call-start = ((), (), s32[]{:S(2)}) async-start(), calls=%async_computation.14 | async-start | bytes 5242880 | tf_op jit(solution)/shard_map/reduce_scatter | solution.py:204
  433.4 58.2 %collective-permute-start.1 = (s32[512]{0:T(512)S(1)}, s32[512]{0:T(512)S(1)}, u32[]{:S(2)}, u32[]{:S(2)}) collective-permute-start(s32[512]{0:T(512)S(1)} %bitcast.536), channel_id=1, source_target_pairs={{0,32},{32,64},{64,96},{96,0},{1,33},{33,65},{65,97},{97,1},{2,34}... | collective-permute-start | bytes 6152 | tf_op jit(solution)/shard_map/ppermute | solution.py:50
  509.2 121.9 %all-gather.14.cloned.1.call-start = ((), (), s32[]{:S(2)}) async-start(), calls=%async_computation.15 | async-start | bytes 5242880 | tf_op jit(solution)/shard_map/all_gather | solution.py:142
  556.4 24.9 %collective-permute-start.2 = (bf16[128,4096]{1,0:T(8,128)(2,1)S(1)}, bf16[128,4096]{1,0:T(8,128)(2,1)S(1)}, u32[]{:S(2)}, u32[]{:S(2)}) collective-permute-start(bf16[128,4096]{1,0:T(8,128)(2,1)S(1)} %fusion.240), channel_id=1, source_target_pairs={{0,32},{32,64},{64,96},{96,0},{1,33},{33,65},{65,97},{97,1},{2,34}... | collective-permute-start | bytes 3145736 | tf_op jit(solution)/shard_map/ppermute | solution.py:50
  583.0 122.9 %reduce-scatter.12.cloned.1.call-start = ((), (), s32[]{:S(2)}) async-start(), calls=%async_computation.16 | async-start | bytes 5242880 | tf_op jit(solution)/shard_map/reduce_scatter | solution.py:204
  583.0 58.2 %collective-permute-start.3 = (s32[512]{0:T(512)S(1)}, s32[512]{0:T(512)S(1)}, u32[]{:S(2)}, u32[]{:S(2)}) collective-permute-start(s32[512]{0:T(512)S(1)} %collective-permute-done.1), channel_id=1, source_target_pairs={{0,32},{32,64},{64,96},{96,0},{1,33},{33,65},{65,97},{97,1},{2,34}... | collective-permute-start | bytes 6152 | tf_op jit(solution)/shard_map/ppermute | solution.py:50
  658.5 123.4 %all-gather.16.cloned.1.call-start = ((), (), s32[]{:S(2)}) async-start(), calls=%async_computation.17 | async-start | bytes 5242880 | tf_op jit(solution)/shard_map/all_gather | solution.py:142
  707.3 24.9 %collective-permute-start.4 = (bf16[128,4096]{1,0:T(8,128)(2,1)S(1)}, bf16[128,4096]{1,0:T(8,128)(2,1)S(1)}, u32[]{:S(2)}, u32[]{:S(2)}) collective-permute-start(bf16[128,4096]{1,0:T(8,128)(2,1)S(1)} %fusion.239), channel_id=1, source_target_pairs={{0,32},{32,64},{64,96},{96,0},{1,33},{33,65},{65,97},{97,1},{2,34}... | collective-permute-start | bytes 3145736 | tf_op jit(solution)/shard_map/ppermute | solution.py:50
  733.9 122.9 %reduce-scatter.14.cloned.1.call-start = ((), (), s32[]{:S(2)}) async-start(), calls=%async_computation.18 | async-start | bytes 5242880 | tf_op jit(solution)/shard_map/reduce_scatter | solution.py:204
  733.9 58.4 %collective-permute-start.5 = (s32[512]{0:T(512)S(1)}, s32[512]{0:T(512)S(1)}, u32[]{:S(2)}, u32[]{:S(2)}) collective-permute-start(s32[512]{0:T(512)S(1)} %collective-permute-done.3), channel_id=1, source_target_pairs={{0,32},{32,64},{64,96},{96,0},{1,33},{33,65},{65,97},{97,1},{2,34}... | collective-permute-start | bytes 6152 | tf_op jit(solution)/shard_map/ppermute | solution.py:50
  809.5 123.4 %all-gather.18.cloned.1.call-start = ((), (), s32[]{:S(2)}) async-start(), calls=%async_computation.19 | async-start | bytes 5242880 | tf_op jit(solution)/shard_map/all_gather | solution.py:142
  858.4 24.9 %collective-permute-start.6 = (bf16[128,4096]{1,0:T(8,128)(2,1)S(1)}, bf16[128,4096]{1,0:T(8,128)(2,1)S(1)}, u32[]{:S(2)}, u32[]{:S(2)}) collective-permute-start(bf16[128,4096]{1,0:T(8,128)(2,1)S(1)} %fusion.238), channel_id=1, source_target_pairs={{0,32},{32,64},{64,96},{96,0},{1,33},{33,65},{65,97},{97,1},{2,34}... | collective-permute-start | bytes 3145736 | tf_op jit(solution)/shard_map/ppermute | solution.py:50
  884.9 122.9 %reduce-scatter.16.cloned.1.call-start = ((), (), s32[]{:S(2)}) async-start(), calls=%async_computation.20 | async-start | bytes 5242880 | tf_op jit(solution)/shard_map/reduce_scatter | solution.py:204
  884.9 58.2 %collective-permute-start.7 = (s32[512]{0:T(512)S(1)}, s32[512]{0:T(512)S(1)}, u32[]{:S(2)}, u32[]{:S(2)}) collective-permute-start(s32[512]{0:T(512)S(1)} %collective-permute-done.5), channel_id=1, source_target_pairs={{0,32},{32,64},{64,96},{96,0},{1,33},{33,65},{65,97},{97,1},{2,34}... | collective-permute-start | bytes 6152 | tf_op jit(solution)/shard_map/ppermute | solution.py:50
  960.5 123.4 %all-gather.20.cloned.1.call-start = ((), (), s32[]{:S(2)}) async-start(), calls=%async_computation.21 | async-start | bytes 5242880 | tf_op jit(solution)/shard_map/all_gather | solution.py:142
  1009.3 24.9 %collective-permute-start.8 = (bf16[128,4096]{1,0:T(8,128)(2,1)S(1)}, bf16[128,4096]{1,0:T(8,128)(2,1)S(1)}, u32[]{:S(2)}, u32[]{:S(2)}) collective-permute-start(bf16[128,4096]{1,0:T(8,128)(2,1)S(1)} %fusion.237), channel_id=1, source_target_pairs={{0,32},{32,64},{64,96},{96,0},{1,33},{33,65},{65,97},{97,1},{2,34}... | collective-permute-start | bytes 3145736 | tf_op jit(solution)/shard_map/ppermute | solution.py:50
  1035.9 122.9 %reduce-scatter.18.cloned.1.call-start = ((), (), s32[]{:S(2)}) async-start(), calls=%async_computation.22 | async-start | bytes 5242880 | tf_op jit(solution)/shard_map/reduce_scatter | solution.py:204
  1035.9 48.9 %collective-permute-start.9 = (s32[512]{0:T(512)S(1)}, s32[512]{0:T(512)S(1)}, u32[]{:S(2)}, u32[]{:S(2)}) collective-permute-start(s32[512]{0:T(512)S(1)} %collective-permute-done.7), channel_id=1, source_target_pairs={{0,32},{32,64},{64,96},{96,0},{1,33},{33,65},{65,97},{97,1},{2,34}... | collective-permute-start | bytes 6152 | tf_op jit(solution)/shard_map/ppermute | solution.py:50
  1088.4 146.5 %all-gather.22.cloned.1.call-start = ((), (), s32[]{:S(2)}) async-start(), calls=%async_computation.23 | async-start | bytes 5242880 | tf_op jit(solution)/shard_map/all_gather | solution.py:142
  1160.3 24.9 %collective-permute-start.10 = (bf16[128,4096]{1,0:T(8,128)(2,1)S(1)}, bf16[128,4096]{1,0:T(8,128)(2,1)S(1)}, u32[]{:S(2)}, u32[]{:S(2)}) collective-permute-start(bf16[128,4096]{1,0:T(8,128)(2,1)S(1)} %fusion.236), channel_id=1, source_target_pairs={{0,32},{32,64},{64,96},{96,0},{1,33},{33,65},{65,97},{97,1},{2,34}... | collective-permute-start | bytes 3145736 | tf_op jit(solution)/shard_map/ppermute | solution.py:50
  1186.8 116.9 %reduce-scatter.20.cloned.1.call-start = ((), (), s32[]{:S(2)}) async-start(), calls=%async_computation.24 | async-start | bytes 5242880 | tf_op jit(solution)/shard_map/reduce_scatter | solution.py:204
  1186.9 48.3 %collective-permute-start.11 = (s32[512]{0:T(512)S(1)}, s32[512]{0:T(512)S(1)}, u32[]{:S(2)}, u32[]{:S(2)}) collective-permute-start(s32[512]{0:T(512)S(1)} %collective-permute-done.9), channel_id=1, source_target_pairs={{0,32},{32,64},{64,96},{96,0},{1,33},{33,65},{65,97},{97,1},{2,34}... | collective-permute-start | bytes 6152 | tf_op jit(solution)/shard_map/ppermute | solution.py:50
  1305.3 24.9 %collective-permute-start.12 = (bf16[128,4096]{1,0:T(8,128)(2,1)S(1)}, bf16[128,4096]{1,0:T(8,128)(2,1)S(1)}, u32[]{:S(2)}, u32[]{:S(2)}) collective-permute-start(bf16[128,4096]{1,0:T(8,128)(2,1)S(1)} %fusion.235), channel_id=1, source_target_pairs={{0,32},{32,64},{64,96},{96,0},{1,33},{33,65},{65,97},{97,1},{2,34}... | collective-permute-start | bytes 3145736 | tf_op jit(solution)/shard_map/ppermute | solution.py:50
  1330.1 49.6 %collective-permute-start.13 = (bf16[128,4096]{1,0:T(8,128)(2,1)S(1)}, bf16[128,4096]{1,0:T(8,128)(2,1)S(1)}, u32[]{:S(2)}, u32[]{:S(2)}) collective-permute-start(bf16[128,4096]{1,0:T(8,128)(2,1)S(1)} %collective-permute-done.12), channel_id=1, source_target_pairs={{0,32},{32,64},{64,96},{96,0},{1,33},{33,65},{65,97},{97,1},{2,34}... | collective-permute-start | bytes 3145736 | tf_op jit(solution)/shard_map/ppermute | solution.py:50
  (26 other events, 291.0 us)
Sparse Core Ops, SparseCore 0:
  13.2 69.3 all-gather.23
  285.6 46.8 all-gather.9
  337.1 67.6 reduce-scatter.7
  433.5 47.9 all-gather.11
  509.3 45.5 reduce-scatter.9
  583.1 47.8 all-gather.13
  658.6 47.1 reduce-scatter.11
  734.0 47.8 all-gather.15
  809.6 47.1 reduce-scatter.13
  885.0 47.9 all-gather.17
  960.6 47.1 reduce-scatter.15
  1036.0 47.8 all-gather.19
  1088.5 70.1 reduce-scatter.17
  1187.0 47.8 all-gather.21
  1237.9 65.7 reduce-scatter.19
where the time goes:
time: 1400 us; the launch traced here: 1390 us
  waiting for transfers between devices  1020 us (73%)
  local copies, waits for them, and re-layouts  106 us (8%)
  matrix products  101 us (7%)
  other arithmetic  51.4 us (4%)
  starting transfers between devices  48.4 us (3%)
  blocking collectives  46.2 us (3%)
  between operations  15.6 us (1%)
    reduce_scatter x7, waiting for transfers between devices, decoder_layer(): lax.psum_scatter(lax.cond(active, out_computed, out_skipped, mixed).astyp...  386 us
    all_gather x7, waiting for transfers between devices, decoder_layer(): piece = lax.all_gather(normed, 'mp', axis=0, tiled=True)  325 us
    ppermute x14, waiting for transfers between devices, shifted(): return lax.ppermute(value, axis, pairs)  163 us
    all_gather x1, waiting for transfers between devices, one_gather(): lines, at, done = (lax.all_gather(flat, axis), 0, [])  66.2 us
    all_to_all x2, waiting for transfers between devices, copy_for_each(): return lax.all_to_all(copies, axis, split_axis=0, concat_axis=0, tiled=True)  59.1 us
    psum x4, blocking collectives, over_axes(): array = lax.psum(array, axis)  46.2 us
  transfers between devices with their start and end apart: 33, of which 26 were waited for; matrix products, arithmetic and copies ran while one was open for 6% of the time, Pallas kernels for 0%

commit v1 on v0

--- a/solution.py
+++ b/solution.py
@@ -16,6 +16,12 @@
 EPS = 1e-05
 ROPE_BASE = 500000.0
 BLOCKED = -1e30
+
+
+def joined_along(parts, dim):
+    parts = jnp.moveaxis(parts, 0, dim)
+    shape = parts.shape
+    return parts.reshape(*shape[:dim], shape[dim] * shape[dim + 1], *shape[dim + 2 :])
 
 
 def copy_for_each(array, axis):
@@ -139,7 +145,19 @@
     pair_width = w_kv.shape[2]
     joined_width = query_width + 2 * pair_width
     model_width = w_out.shape[1]
-    piece = lax.all_gather(normed, "mp", axis=0, tiled=True)
+    size = lax.axis_size("mp")
+    pairs_2 = [(i, (i + 1) % size) for i in range(size)]
+    back = [(b, a_2) for a_2, b in pairs_2]
+    lower, upper = ([], [])
+    for step in range(size - 1):
+        if step % 2 == 0:
+            lower.append(lax.ppermute(lower[-1] if lower else normed, "mp", pairs_2))
+        else:
+            upper.append(lax.ppermute(upper[-1] if upper else normed, "mp", back))
+    blocks_2 = jnp.stack([*lower[::-1], normed, *upper])
+    shift = lax.axis_index("mp") - len(lower)
+    blocks_2 = blocks_2[(jnp.arange(size) - shift) % size]
+    piece = joined_along(blocks_2, 0)
     row_count = piece.shape[0]
 
     def project_computed(rows):

time: 1400 us -> 1460 us (1.043)
  other arithmetic: 51.4 us -> 78.1 us
  local copies, waits for them, and re-layouts: 106 us -> 128 us
  starting transfers between devices: 48.4 us -> 65.3 us
    all_gather x7 -> x0, waiting for transfers between devices: 325 us -> none  [decoder_layer(): piece = lax.all_gather(normed, 'mp', axis=0, tiled=True)]
    ppermute x0 -> x21, waiting for transfers between devices: none -> 303 us  [the longest x14 301 us: decoder_layer(): lower.append(lax.ppermute(lower[-1] if lower else normed, 'mp', pairs_2))]
    another operation x8 -> x21, other arithmetic: 2.98 us -> 30.7 us  [the longest x13 27.8 us: decoder_layer(): blocks_2 = jnp.stack([*lower[::-1], normed, *upper])]
    ppermute x0 -> x21, starting transfers between devices: none -> 22.9 us  [the longest x7 20.6 us: decoder_layer(): upper.append(lax.ppermute(upper[-1] if upper else normed, 'mp', back))]
    gather x0 -> x4, local copies, waits for them, and re-layouts: none -> 20 us  [decoder_layer(): blocks_2 = blocks_2[(jnp.arange(size) - shift) % size]]
  transfers between devices with their start and end apart: 33 -> 47, of which waited for: 26 -> 34; matrix products, arithmetic and copies ran while one was open for 6% -> 10% of each run, Pallas kernels for 0% -> 0%
where the time goes in v1:
time: 1460 us; the launch traced here: 1450 us
  waiting for transfers between devices  1010 us (69%)
  local copies, waits for them, and re-layouts  128 us (9%)
  matrix products  105 us (7%)
  other arithmetic  78.1 us (5%)
  starting transfers between devices  65.3 us (4%)
  blocking collectives  46.2 us (3%)
  between operations  15.7 us (1%)
    reduce_scatter x7, waiting for transfers between devices, decoder_layer(): lax.psum_scatter(lax.cond(active, out_computed, out_skipped, mixed).astyp...  398 us
    ppermute x14, waiting for transfers between devices, decoder_layer(): lower.append(lax.ppermute(lower[-1] if lower else normed, 'mp', pairs_2))  301 us
    ppermute x14, waiting for transfers between devices, shifted(): return lax.ppermute(value, axis, pairs)  163 us
    all_gather x1, waiting for transfers between devices, one_gather(): lines, at, done = (lax.all_gather(flat, axis), 0, [])  66.2 us
    all_to_all x2, waiting for transfers between devices, copy_for_each(): return lax.all_to_all(copies, axis, split_axis=0, concat_axis=0, tiled=True)  59.1 us
    psum x4, blocking collectives, over_axes(): array = lax.psum(array, axis)  46.2 us
  transfers between devices with their start and end apart: 47, of which 34 were waited for; matrix products, arithmetic and copies ran while one was open for 10% of the time, Pallas kernels for 0%

profile of v1, /device:TPU:32, one launch (start us, length us, event | category | flops | bytes accessed | tf_op | source)
XLA Modules:
  0.0 1448.3 jit_solution(13929155473218523133)
XLA Ops:
  16.4 66.2 %all-gather.3.cloned.1.call-done = bf16[7340032]{0:T(1024)(128)(2,1)} async-done(((bf16[229376]{0:T(1024)(128)(2,1)}), bf16[7340032]{0:T(1024)(128)(2,1)}) %all-gather.3.cloned.1.call-update) | async-done | bytes 14680080 | tf_op jit(solution)/shard_map/all_gather | solution.py:45
  141.2 27.2 %all-to-all-done = bf16[4,512,1024]{2,1,0:T(8,128)(2,1)} async-done(((bf16[4,512,1024]{2,1,0:T(8,128)(2,1)}), bf16[4,512,1024]{2,1,0:T(8,128)(2,1)}, u32[]{:S(2)}, u32[]{:S(2)}) %all-to-all-start) | async-done | bytes 4194336 | tf_op jit(solution)/shard_map/all_to_all | solution.py:29
  205.7 31.9 %all-to-all-done.1 = bf16[4,512,1024]{2,1,0:T(8,128)(2,1)} async-done(((bf16[4,512,1024]{2,1,0:T(8,128)(2,1)}), bf16[4,512,1024]{2,1,0:T(8,128)(2,1)}, u32[]{:S(2)}, u32[]{:S(2)}) %all-to-all-start.1) | async-done | bytes 4194336 | tf_op jit(solution)/shard_map/all_to_all | solution.py:29
  309.1 16.8 %collective-permute-done.1 = bf16[128,4096]{1,0:T(8,128)(2,1)} collective-permute-done((bf16[128,4096]{1,0:T(8,128)(2,1)}, bf16[128,4096]{1,0:T(8,128)(2,1)}, u32[]{:S(2)}, u32[]{:S(2)}) %collective-permute-start.1) | collective-permute-done | bytes 1048608 | tf_op jit(solution)/shard_map/ppermute | solution.py:154
  334.5 72.8 %reduce-scatter.8.cloned.1.call-done = bf16[128,4096]{1,0:T(8,128)(2,1)} async-done(((bf16[512,4096]{1,0:T(8,128)(2,1)}), bf16[128,4096]{1,0:T(8,128)(2,1)}) %reduce-scatter.8.cloned.1.call-update) | async-done | bytes 1048592 | tf_op jit(solution)/shard_map/reduce_scatter | solution.py:222
  411.1 23.3 %collective-permute-done.3 = bf16[128,4096]{1,0:T(8,128)(2,1)S(1)} collective-permute-done((bf16[128,4096]{1,0:T(8,128)(2,1)S(1)}, bf16[128,4096]{1,0:T(8,128)(2,1)S(1)}, u32[]{:S(2)}, u32[]{:S(2)}) %collective-permute-start.3) | collective-permute-done | bytes 1048608 | tf_op jit(solution)/shard_map/ppermute | solution.py:56
  439.2 22.3 %collective-permute-done.5 = bf16[128,4096]{1,0:T(8,128)(2,1)} collective-permute-done((bf16[128,4096]{1,0:T(8,128)(2,1)}, bf16[128,4096]{1,0:T(8,128)(2,1)}, u32[]{:S(2)}, u32[]{:S(2)}) %collective-permute-start.5) | collective-permute-done | bytes 1048608 | tf_op jit(solution)/shard_map/ppermute | solution.py:154
  463.3 22.8 %collective-permute-done.6 = bf16[128,4096]{1,0:T(8,128)(2,1)} collective-permute-done((bf16[128,4096]{1,0:T(8,128)(2,1)}, bf16[128,4096]{1,0:T(8,128)(2,1)}, u32[]{:S(2)}, u32[]{:S(2)}) %collective-permute-start.6) | collective-permute-done | bytes 1048608 | tf_op jit(solution)/shard_map/ppermute | solution.py:154
  522.7 44.3 %reduce-scatter.10.cloned.1.call-done = bf16[128,4096]{1,0:T(8,128)(2,1)} async-done(((bf16[512,4096]{1,0:T(8,128)(2,1)}), bf16[128,4096]{1,0:T(8,128)(2,1)}) %reduce-scatter.10.cloned.1.call-update) | async-done | bytes 1048592 | tf_op jit(solution)/shard_map/reduce_scatter | solution.py:222
  570.2 23.3 %collective-permute-done.8 = bf16[128,4096]{1,0:T(8,128)(2,1)S(1)} collective-permute-done((bf16[128,4096]{1,0:T(8,128)(2,1)S(1)}, bf16[128,4096]{1,0:T(8,128)(2,1)S(1)}, u32[]{:S(2)}, u32[]{:S(2)}) %collective-permute-start.8) | collective-permute-done | bytes 1048608 | tf_op jit(solution)/shard_map/ppermute | solution.py:56
  598.3 22.3 %collective-permute-done.10 = bf16[128,4096]{1,0:T(8,128)(2,1)} collective-permute-done((bf16[128,4096]{1,0:T(8,128)(2,1)}, bf16[128,4096]{1,0:T(8,128)(2,1)}, u32[]{:S(2)}, u32[]{:S(2)}) %collective-permute-start.10) | collective-permute-done | bytes 1048608 | tf_op jit(solution)/shard_map/ppermute | solution.py:154
  622.5 22.8 %collective-permute-done.11 = bf16[128,4096]{1,0:T(8,128)(2,1)} collective-permute-done((bf16[128,4096]{1,0:T(8,128)(2,1)}, bf16[128,4096]{1,0:T(8,128)(2,1)}, u32[]{:S(2)}, u32[]{:S(2)}) %collective-permute-start.11) | collective-permute-done | bytes 1048608 | tf_op jit(solution)/shard_map/ppermute | solution.py:154
  682.3 45.3 %reduce-scatter.12.cloned.1.call-done = bf16[128,4096]{1,0:T(8,128)(2,1)} async-done(((bf16[512,4096]{1,0:T(8,128)(2,1)}), bf16[128,4096]{1,0:T(8,128)(2,1)}) %reduce-scatter.12.cloned.1.call-update) | async-done | bytes 1048592 | tf_op jit(solution)/shard_map/reduce_scatter | solution.py:222
  730.7 23.3 %collective-permute-done.13 = bf16[128,4096]{1,0:T(8,128)(2,1)S(1)} collective-permute-done((bf16[128,4096]{1,0:T(8,128)(2,1)S(1)}, bf16[128,4096]{1,0:T(8,128)(2,1)S(1)}, u32[]{:S(2)}, u32[]{:S(2)}) %collective-permute-start.13) | collective-permute-done | bytes 1048608 | tf_op jit(solution)/shard_map/ppermute | solution.py:56
  758.8 22.3 %collective-permute-done.15 = bf16[128,4096]{1,0:T(8,128)(2,1)} collective-permute-done((bf16[128,4096]{1,0:T(8,128)(2,1)}, bf16[128,4096]{1,0:T(8,128)(2,1)}, u32[]{:S(2)}, u32[]{:S(2)}) %collective-permute-start.15) | collective-permute-done | bytes 1048608 | tf_op jit(solution)/shard_map/ppermute | solution.py:154
  783.0 22.8 %collective-permute-done.16 = bf16[128,4096]{1,0:T(8,128)(2,1)} collective-permute-done((bf16[128,4096]{1,0:T(8,128)(2,1)}, bf16[128,4096]{1,0:T(8,128)(2,1)}, u32[]{:S(2)}, u32[]{:S(2)}) %collective-permute-start.16) | collective-permute-done | bytes 1048608 | tf_op jit(solution)/shard_map/ppermute | solution.py:154
  842.3 45.7 %reduce-scatter.14.cloned.1.call-done = bf16[128,4096]{1,0:T(8,128)(2,1)} async-done(((bf16[512,4096]{1,0:T(8,128)(2,1)}), bf16[128,4096]{1,0:T(8,128)(2,1)}) %reduce-scatter.14.cloned.1.call-update) | async-done | bytes 1048592 | tf_op jit(solution)/shard_map/reduce_scatter | solution.py:222
  891.2 23.3 %collective-permute-done.18 = bf16[128,4096]{1,0:T(8,128)(2,1)S(1)} collective-permute-done((bf16[128,4096]{1,0:T(8,128)(2,1)S(1)}, bf16[128,4096]{1,0:T(8,128)(2,1)S(1)}, u32[]{:S(2)}, u32[]{:S(2)}) %collective-permute-start.18) | collective-permute-done | bytes 1048608 | tf_op jit(solution)/shard_map/ppermute | solution.py:56
  919.3 22.3 %collective-permute-done.20 = bf16[128,4096]{1,0:T(8,128)(2,1)} collective-permute-done((bf16[128,4096]{1,0:T(8,128)(2,1)}, bf16[128,4096]{1,0:T(8,128)(2,1)}, u32[]{:S(2)}, u32[]{:S(2)}) %collective-permute-start.20) | collective-permute-done | bytes 1048608 | tf_op jit(solution)/shard_map/ppermute | solution.py:154
  943.5 22.8 %collective-permute-done.21 = bf16[128,4096]{1,0:T(8,128)(2,1)} collective-permute-done((bf16[128,4096]{1,0:T(8,128)(2,1)}, bf16[128,4096]{1,0:T(8,128)(2,1)}, u32[]{:S(2)}, u32[]{:S(2)}) %collective-permute-start.21) | collective-permute-done | bytes 1048608 | tf_op jit(solution)/shard_map/ppermute | solution.py:154
  969.9 16.5 %conditional.33 = (bf16[512,768]{0,1:T(8,128)(2,1)}) conditional(s32[]{:T(128)} %convert_element_type.549, () %tuple.160, (bf16[4,128,4096]{2,1,0:T(8,128)(2,1)}, s32[4,1]{0,1:T(1,128)S(1)}, bf16[4096,512]{0,1:T(8,128)(2,1)}, bf16[2,4096,128]{2,1,0:T(8,128)(2,1)S(1)}) %tuple.347), branch_computations={%region_54.55_spmd, %region_55.56_spmd} | conditional | flops 3226338816 | bytes 50867012 | solution.py:184
  1003.2 45.3 %reduce-scatter.16.cloned.1.call-done = bf16[128,4096]{1,0:T(8,128)(2,1)} async-done(((bf16[512,4096]{1,0:T(8,128)(2,1)}), bf16[128,4096]{1,0:T(8,128)(2,1)}) %reduce-scatter.16.cloned.1.call-update) | async-done | bytes 1048592 | tf_op jit(solution)/shard_map/reduce_scatter | solution.py:222
  1051.7 23.3 %collective-permute-done.23 = bf16[128,4096]{1,0:T(8,128)(2,1)S(1)} collective-permute-done((bf16[128,4096]{1,0:T(8,128)(2,1)S(1)}, bf16[128,4096]{1,0:T(8,128)(2,1)S(1)}, u32[]{:S(2)}, u32[]{:S(2)}) %collective-permute-start.23) | collective-permute-done | bytes 1048608 | tf_op jit(solution)/shard_map/ppermute | solution.py:56
  1079.8 22.3 %collective-permute-done.25 = bf16[128,4096]{1,0:T(8,128)(2,1)} collective-permute-done((bf16[128,4096]{1,0:T(8,128)(2,1)}, bf16[128,4096]{1,0:T(8,128)(2,1)}, u32[]{:S(2)}, u32[]{:S(2)}) %collective-permute-start.25) | collective-permute-done | bytes 1048608 | tf_op jit(solution)/shard_map/ppermute | solution.py:154
  1104.0 22.8 %collective-permute-done.26 = bf16[128,4096]{1,0:T(8,128)(2,1)} collective-permute-done((bf16[128,4096]{1,0:T(8,128)(2,1)}, bf16[128,4096]{1,0:T(8,128)(2,1)}, u32[]{:S(2)}, u32[]{:S(2)}) %collective-permute-start.26) | collective-permute-done | bytes 1048608 | tf_op jit(solution)/shard_map/ppermute | solution.py:154
  1135.0 74.0 %reduce-scatter.18.cloned.1.call-done = bf16[128,4096]{1,0:T(8,128)(2,1)} async-done(((bf16[512,4096]{1,0:T(8,128)(2,1)}), bf16[128,4096]{1,0:T(8,128)(2,1)}) %reduce-scatter.18.cloned.1.call-update) | async-done | bytes 1048592 | tf_op jit(solution)/shard_map/reduce_scatter | solution.py:222
  1212.1 23.3 %collective-permute-done.28 = bf16[128,4096]{1,0:T(8,128)(2,1)S(1)} collective-permute-done((bf16[128,4096]{1,0:T(8,128)(2,1)S(1)}, bf16[128,4096]{1,0:T(8,128)(2,1)S(1)}, u32[]{:S(2)}, u32[]{:S(2)}) %collective-permute-start.28) | collective-permute-done | bytes 1048608 | tf_op jit(solution)/shard_map/ppermute | solution.py:56
  1240.3 22.3 %collective-permute-done.30 = bf16[128,4096]{1,0:T(8,128)(2,1)} collective-permute-done((bf16[128,4096]{1,0:T(8,128)(2,1)}, bf16[128,4096]{1,0:T(8,128)(2,1)}, u32[]{:S(2)}, u32[]{:S(2)}) %collective-permute-start.30) | collective-permute-done | bytes 1048608 | tf_op jit(solution)/shard_map/ppermute | solution.py:154
  1264.5 22.7 %collective-permute-done.31 = bf16[128,4096]{1,0:T(8,128)(2,1)} collective-permute-done((bf16[128,4096]{1,0:T(8,128)(2,1)}, bf16[128,4096]{1,0:T(8,128)(2,1)}, u32[]{:S(2)}, u32[]{:S(2)}) %collective-permute-start.31) | collective-permute-done | bytes 1048608 | tf_op jit(solution)/shard_map/ppermute | solution.py:154
  1293.8 70.5 %reduce-scatter.20.cloned.1.call-done = bf16[128,4096]{1,0:T(8,128)(2,1)} async-done(((bf16[512,4096]{1,0:T(8,128)(2,1)}), bf16[128,4096]{1,0:T(8,128)(2,1)}) %reduce-scatter.20.cloned.1.call-update) | async-done | bytes 1048592 | tf_op jit(solution)/shard_map/reduce_scatter | solution.py:222
  1367.4 23.3 %collective-permute-done.33 = bf16[128,4096]{1,0:T(8,128)(2,1)S(1)} collective-permute-done((bf16[128,4096]{1,0:T(8,128)(2,1)S(1)}, bf16[128,4096]{1,0:T(8,128)(2,1)S(1)}, u32[]{:S(2)}, u32[]{:S(2)}) %collective-permute-start.33) | collective-permute-done | bytes 1048608 | tf_op jit(solution)/shard_map/ppermute | solution.py:56
  1392.9 26.3 %psum.28 = s32[]{:T(128)} all-reduce(s32[]{:T(128)} %reduce_sum.242), channel_id=1, replica_groups=mesh['section'=4,'dp_0'=4,'dp_1'=2,'mp'=4] {'section'}, use_global_device_ids=true, to_apply=%region_84.85 | all-reduce | flops 1 | bytes 8 | tf_op jit(solution)/shard_map/psum | solution.py:61
  (349 shorter events, 557.7 us)
Async XLA Ops:
  7.2 75.4 %all-gather.3.cloned.1.call-start = ((), (), s32[]{:S(2)}) async-start(), calls=%async_computation.18 | async-start | bytes 15138816 | tf_op jit(solution)/shard_map/all_gather | solution.py:45
  113.6 54.8 %all-to-all-start = ((bf16[4,512,1024]{2,1,0:T(8,128)(2,1)}), bf16[4,512,1024]{2,1,0:T(8,128)(2,1)}, u32[]{:S(2)}, u32[]{:S(2)}) async-start(bf16[4,512,1024]{2,1,0:T(8,128)(2,1)} %broadcast_in_dim.78), calls=%async_computation | async-start | bytes 8388608 | tf_op jit(solution)/shard_map/all_to_all | solution.py:29
  183.8 53.8 %all-to-all-start.1 = ((bf16[4,512,1024]{2,1,0:T(8,128)(2,1)}), bf16[4,512,1024]{2,1,0:T(8,128)(2,1)}, u32[]{:S(2)}, u32[]{:S(2)}) async-start(bf16[4,512,1024]{2,1,0:T(8,128)(2,1)} %broadcast_in_dim.87), calls=%async_computation.1 | async-start | bytes 8388608 | tf_op jit(solution)/shard_map/all_to_all | solution.py:29
  266.1 141.2 %reduce-scatter.8.cloned.1.call-start = ((), (), s32[]{:S(2)}) async-start(), calls=%async_computation.11 | async-start | bytes 5242880 | tf_op jit(solution)/shard_map/reduce_scatter | solution.py:222
  334.5 232.5 %reduce-scatter.10.cloned.1.call-start = ((), (), s32[]{:S(2)}) async-start(), calls=%async_computation.12 | async-start | bytes 5242880 | tf_op jit(solution)/shard_map/reduce_scatter | solution.py:222
  409.4 24.9 %collective-permute-start.3 = (bf16[128,4096]{1,0:T(8,128)(2,1)S(1)}, bf16[128,4096]{1,0:T(8,128)(2,1)S(1)}, u32[]{:S(2)}, u32[]{:S(2)}) collective-permute-start(bf16[128,4096]{1,0:T(8,128)(2,1)S(1)} %fusion.241), channel_id=1, source_target_pairs={{0,32},{32,64},{64,96},{96,0},{1,33},{33,65},{65,97},{97,1},{2,34}... | collective-permute-start | bytes 3145736 | tf_op jit(solution)/shard_map/ppermute | solution.py:56
  436.0 25.5 %collective-permute-start.5 = (bf16[128,4096]{1,0:T(8,128)(2,1)}, bf16[128,4096]{1,0:T(8,128)(2,1)}, u32[]{:S(2)}, u32[]{:S(2)}) collective-permute-start(bf16[128,4096]{1,0:T(8,128)(2,1)} %fusion.205), channel_id=1, source_target_pairs={{0,1},{1,2},{2,3},{3,0},{4,5},{5,6},{6,7},{7,4},{8,9},{9,10},{10,1... | collective-permute-start | bytes 3145736 | tf_op jit(solution)/shard_map/ppermute | solution.py:154
  436.2 27.1 %collective-permute-start.7 = (bf16[128,4096]{1,0:T(8,128)(2,1)}, bf16[128,4096]{1,0:T(8,128)(2,1)}, u32[]{:S(2)}, u32[]{:S(2)}) collective-permute-start(bf16[128,4096]{1,0:T(8,128)(2,1)} %fusion.205), channel_id=1, source_target_pairs={{1,0},{2,1},{3,2},{0,3},{5,4},{6,5},{7,6},{4,7},{9,8},{10,9},{11,1... | collective-permute-start | bytes 3145736 | tf_op jit(solution)/shard_map/ppermute | solution.py:156
  461.5 44.7 %collective-permute-start.4 = (s32[512]{0:T(512)S(1)}, s32[512]{0:T(512)S(1)}, u32[]{:S(2)}, u32[]{:S(2)}) collective-permute-start(s32[512]{0:T(512)S(1)} %bitcast.653), channel_id=1, source_target_pairs={{0,32},{32,64},{64,96},{96,0},{1,33},{33,65},{65,97},{97,1},{2,34}... | collective-permute-start | bytes 6152 | tf_op jit(solution)/shard_map/ppermute | solution.py:56
  522.6 204.9 %reduce-scatter.12.cloned.1.call-start = ((), (), s32[]{:S(2)}) async-start(), calls=%async_computation.13 | async-start | bytes 5242880 | tf_op jit(solution)/shard_map/reduce_scatter | solution.py:222
  568.6 24.9 %collective-permute-start.8 = (bf16[128,4096]{1,0:T(8,128)(2,1)S(1)}, bf16[128,4096]{1,0:T(8,128)(2,1)S(1)}, u32[]{:S(2)}, u32[]{:S(2)}) collective-permute-start(bf16[128,4096]{1,0:T(8,128)(2,1)S(1)} %fusion.240), channel_id=1, source_target_pairs={{0,32},{32,64},{64,96},{96,0},{1,33},{33,65},{65,97},{97,1},{2,34}... | collective-permute-start | bytes 3145736 | tf_op jit(solution)/shard_map/ppermute | solution.py:56
  595.1 25.5 %collective-permute-start.10 = (bf16[128,4096]{1,0:T(8,128)(2,1)}, bf16[128,4096]{1,0:T(8,128)(2,1)}, u32[]{:S(2)}, u32[]{:S(2)}) collective-permute-start(bf16[128,4096]{1,0:T(8,128)(2,1)} %fusion.209), channel_id=1, source_target_pairs={{0,1},{1,2},{2,3},{3,0},{4,5},{5,6},{6,7},{7,4},{8,9},{9,10},{10,1... | collective-permute-start | bytes 3145736 | tf_op jit(solution)/shard_map/ppermute | solution.py:154
  595.3 27.2 %collective-permute-start.12 = (bf16[128,4096]{1,0:T(8,128)(2,1)}, bf16[128,4096]{1,0:T(8,128)(2,1)}, u32[]{:S(2)}, u32[]{:S(2)}) collective-permute-start(bf16[128,4096]{1,0:T(8,128)(2,1)} %fusion.209), channel_id=1, source_target_pairs={{1,0},{2,1},{3,2},{0,3},{5,4},{6,5},{7,6},{4,7},{9,8},{10,9},{11,1... | collective-permute-start | bytes 3145736 | tf_op jit(solution)/shard_map/ppermute | solution.py:156
  620.6 44.9 %collective-permute-start.9 = (s32[512]{0:T(512)S(1)}, s32[512]{0:T(512)S(1)}, u32[]{:S(2)}, u32[]{:S(2)}) collective-permute-start(s32[512]{0:T(512)S(1)} %collective-permute-done.4), channel_id=1, source_target_pairs={{0,32},{32,64},{64,96},{96,0},{1,33},{33,65},{65,97},{97,1},{2,34}... | collective-permute-start | bytes 6152 | tf_op jit(solution)/shard_map/ppermute | solution.py:56
  681.8 206.2 %reduce-scatter.14.cloned.1.call-start = ((), (), s32[]{:S(2)}) async-start(), calls=%async_computation.14 | async-start | bytes 5242880 | tf_op jit(solution)/shard_map/reduce_scatter | solution.py:222
  755.6 25.5 %collective-permute-start.15 = (bf16[128,4096]{1,0:T(8,128)(2,1)}, bf16[128,4096]{1,0:T(8,128)(2,1)}, u32[]{:S(2)}, u32[]{:S(2)}) collective-permute-start(bf16[128,4096]{1,0:T(8,128)(2,1)} %fusion.213), channel_id=1, source_target_pairs={{0,1},{1,2},{2,3},{3,0},{4,5},{5,6},{6,7},{7,4},{8,9},{9,10},{10,1... | collective-permute-start | bytes 3145736 | tf_op jit(solution)/shard_map/ppermute | solution.py:154
  755.9 27.1 %collective-permute-start.17 = (bf16[128,4096]{1,0:T(8,128)(2,1)}, bf16[128,4096]{1,0:T(8,128)(2,1)}, u32[]{:S(2)}, u32[]{:S(2)}) collective-permute-start(bf16[128,4096]{1,0:T(8,128)(2,1)} %fusion.213), channel_id=1, source_target_pairs={{1,0},{2,1},{3,2},{0,3},{5,4},{6,5},{7,6},{4,7},{9,8},{10,9},{11,1... | collective-permute-start | bytes 3145736 | tf_op jit(solution)/shard_map/ppermute | solution.py:156
  781.1 44.6 %collective-permute-start.14 = (s32[512]{0:T(512)S(1)}, s32[512]{0:T(512)S(1)}, u32[]{:S(2)}, u32[]{:S(2)}) collective-permute-start(s32[512]{0:T(512)S(1)} %collective-permute-done.9), channel_id=1, source_target_pairs={{0,32},{32,64},{64,96},{96,0},{1,33},{33,65},{65,97},{97,1},{2,34}... | collective-permute-start | bytes 6152 | tf_op jit(solution)/shard_map/ppermute | solution.py:56
  842.2 206.3 %reduce-scatter.16.cloned.1.call-start = ((), (), s32[]{:S(2)}) async-start(), calls=%async_computation.15 | async-start | bytes 5242880 | tf_op jit(solution)/shard_map/reduce_scatter | solution.py:222
  889.5 24.9 %collective-permute-start.18 = (bf16[128,4096]{1,0:T(8,128)(2,1)S(1)}, bf16[128,4096]{1,0:T(8,128)(2,1)S(1)}, u32[]{:S(2)}, u32[]{:S(2)}) collective-permute-start(bf16[128,4096]{1,0:T(8,128)(2,1)S(1)} %fusion.238), channel_id=1, source_target_pairs={{0,32},{32,64},{64,96},{96,0},{1,33},{33,65},{65,97},{97,1},{2,34}... | collective-permute-start | bytes 3145736 | tf_op jit(solution)/shard_map/ppermute | solution.py:56
  916.1 25.5 %collective-permute-start.20 = (bf16[128,4096]{1,0:T(8,128)(2,1)}, bf16[128,4096]{1,0:T(8,128)(2,1)}, u32[]{:S(2)}, u32[]{:S(2)}) collective-permute-start(bf16[128,4096]{1,0:T(8,128)(2,1)} %fusion.217), channel_id=1, source_target_pairs={{0,1},{1,2},{2,3},{3,0},{4,5},{5,6},{6,7},{7,4},{8,9},{9,10},{10,1... | collective-permute-start | bytes 3145736 | tf_op jit(solution)/shard_map/ppermute | solution.py:154
  916.3 27.1 %collective-permute-start.22 = (bf16[128,4096]{1,0:T(8,128)(2,1)}, bf16[128,4096]{1,0:T(8,128)(2,1)}, u32[]{:S(2)}, u32[]{:S(2)}) collective-permute-start(bf16[128,4096]{1,0:T(8,128)(2,1)} %fusion.217), channel_id=1, source_target_pairs={{1,0},{2,1},{3,2},{0,3},{5,4},{6,5},{7,6},{4,7},{9,8},{10,9},{11,1... | collective-permute-start | bytes 3145736 | tf_op jit(solution)/shard_map/ppermute | solution.py:156
  941.6 44.9 %collective-permute-start.19 = (s32[512]{0:T(512)S(1)}, s32[512]{0:T(512)S(1)}, u32[]{:S(2)}, u32[]{:S(2)}) collective-permute-start(s32[512]{0:T(512)S(1)} %collective-permute-done.14), channel_id=1, source_target_pairs={{0,32},{32,64},{64,96},{96,0},{1,33},{33,65},{65,97},{97,1},{2,34}... | collective-permute-start | bytes 6152 | tf_op jit(solution)/shard_map/ppermute | solution.py:56
  1002.8 206.2 %reduce-scatter.18.cloned.1.call-start = ((), (), s32[]{:S(2)}) async-start(), calls=%async_computation.16 | async-start | bytes 5242880 | tf_op jit(solution)/shard_map/reduce_scatter | solution.py:222
  1076.6 25.5 %collective-permute-start.25 = (bf16[128,4096]{1,0:T(8,128)(2,1)}, bf16[128,4096]{1,0:T(8,128)(2,1)}, u32[]{:S(2)}, u32[]{:S(2)}) collective-permute-start(bf16[128,4096]{1,0:T(8,128)(2,1)} %fusion.221), channel_id=1, source_target_pairs={{0,1},{1,2},{2,3},{3,0},{4,5},{5,6},{6,7},{7,4},{8,9},{9,10},{10,1... | collective-permute-start | bytes 3145736 | tf_op jit(solution)/shard_map/ppermute | solution.py:154
  1076.8 27.2 %collective-permute-start.27 = (bf16[128,4096]{1,0:T(8,128)(2,1)}, bf16[128,4096]{1,0:T(8,128)(2,1)}, u32[]{:S(2)}, u32[]{:S(2)}) collective-permute-start(bf16[128,4096]{1,0:T(8,128)(2,1)} %fusion.221), channel_id=1, source_target_pairs={{1,0},{2,1},{3,2},{0,3},{5,4},{6,5},{7,6},{4,7},{9,8},{10,9},{11,1... | collective-permute-start | bytes 3145736 | tf_op jit(solution)/shard_map/ppermute | solution.py:156
  1102.1 29.3 %collective-permute-start.24 = (s32[512]{0:T(512)S(1)}, s32[512]{0:T(512)S(1)}, u32[]{:S(2)}, u32[]{:S(2)}) collective-permute-start(s32[512]{0:T(512)S(1)} %collective-permute-done.19), channel_id=1, source_target_pairs={{0,32},{32,64},{64,96},{96,0},{1,33},{33,65},{65,97},{97,1},{2,34}... | collective-permute-start | bytes 6152 | tf_op jit(solution)/shard_map/ppermute | solution.py:56
  1135.0 229.3 %reduce-scatter.20.cloned.1.call-start = ((), (), s32[]{:S(2)}) async-start(), calls=%async_computation.17 | async-start | bytes 5242880 | tf_op jit(solution)/shard_map/reduce_scatter | solution.py:222
  1237.0 25.5 %collective-permute-start.30 = (bf16[128,4096]{1,0:T(8,128)(2,1)}, bf16[128,4096]{1,0:T(8,128)(2,1)}, u32[]{:S(2)}, u32[]{:S(2)}) collective-permute-start(bf16[128,4096]{1,0:T(8,128)(2,1)} %fusion.225), channel_id=1, source_target_pairs={{0,1},{1,2},{2,3},{3,0},{4,5},{5,6},{6,7},{7,4},{8,9},{9,10},{10,1... | collective-permute-start | bytes 3145736 | tf_op jit(solution)/shard_map/ppermute | solution.py:154
  1237.3 27.2 %collective-permute-start.32 = (bf16[128,4096]{1,0:T(8,128)(2,1)}, bf16[128,4096]{1,0:T(8,128)(2,1)}, u32[]{:S(2)}, u32[]{:S(2)}) collective-permute-start(bf16[128,4096]{1,0:T(8,128)(2,1)} %fusion.225), channel_id=1, source_target_pairs={{1,0},{2,1},{3,2},{0,3},{5,4},{6,5},{7,6},{4,7},{9,8},{10,9},{11,1... | collective-permute-start | bytes 3145736 | tf_op jit(solution)/shard_map/ppermute | solution.py:156
  1262.6 28.6 %collective-permute-start.29 = (s32[512]{0:T(512)S(1)}, s32[512]{0:T(512)S(1)}, u32[]{:S(2)}, u32[]{:S(2)}) collective-permute-start(s32[512]{0:T(512)S(1)} %collective-permute-done.24), channel_id=1, source_target_pairs={{0,32},{32,64},{64,96},{96,0},{1,33},{33,65},{65,97},{97,1},{2,34}... | collective-permute-start | bytes 6152 | tf_op jit(solution)/shard_map/ppermute | solution.py:56
  1390.7 49.5 %collective-permute-start.34 = (bf16[128,4096]{1,0:T(8,128)(2,1)S(1)}, bf16[128,4096]{1,0:T(8,128)(2,1)S(1)}, u32[]{:S(2)}, u32[]{:S(2)}) collective-permute-start(bf16[128,4096]{1,0:T(8,128)(2,1)S(1)} %collective-permute-done.33), channel_id=1, source_target_pairs={{0,32},{32,64},{64,96},{96,0},{1,33},{33,65},{65,97},{97,1},{2,34}... | collective-permute-start | bytes 3145736 | tf_op jit(solution)/shard_map/ppermute | solution.py:56
  (36 other events, 568.0 us)
Sparse Core Ops, SparseCore 0:
  13.2 69.3 all-gather.2
  334.6 72.6 reduce-scatter.7
  522.7 44.2 reduce-scatter.9
  681.9 45.5 reduce-scatter.11
  842.4 45.5 reduce-scatter.13
  1002.9 45.5 reduce-scatter.15
  1135.1 73.8 reduce-scatter.17
  1293.9 70.3 reduce-scatter.19
